TPU v7x, 32 devices: a whole 2x2x4 slice. The times are simulated.
32 devices in a mesh: gx: 4 (over y, core), gy: 8 (over z, x).
Axes of the slice: x: 2, y: 2, z: 4, core: 2. Of those that a mesh axis runs over, the one named last changes fastest.
Arguments:
- disp: float32 [3, 32, 128, 128], P(None, 'gx', 'gy'), may hold values from -3 to 3
- vel: float32 [3, 32, 128, 128], P(None, 'gx', 'gy'), may hold values from -30 to 30
- load: float32 [3, 32, 128, 128], P(None, 'gx', 'gy'), may hold values from -96 to 96
- flags: int32 [32, 128, 128], P('gx', 'gy'), may hold values 0 or 1
- mask_bits: int32 [4, 32, 128, 128], P(None, 'gx', 'gy'), may hold values from 0 to 2147483647, as said below
Outputs:
- disp_out: float32 [3, 32, 128, 128], P(None, 'gx', 'gy')
- vel_out: float32 [3, 32, 128, 128], P(None, 'gx', 'gy')
Inputs may be any that keep to these rules, and one draw needn't show every extreme that they name: `mask_bits`: bit b (0 to 30) of word w marks the cell's bond to neighbour number 31 w + b as broken; bit 31, and bits of numbers 122 and above, are zero.
All inputs are finite; a program needn't handle non-finite values. No bound on the sum of `flags` on one device may be relied on, other than what follows from the above.
Results may differ from a plain program's by a relative error of at most 0.0001.
Values sent between devices are 32-bit elements; how exact they have to be, the bound alone decides.
A program may use at most 128 MiB of HBM per device.

v0:
```python
import math

import jax
import jax.numpy as jnp
from jax import lax
from jax.sharding import PartitionSpec as P

ITERS = 8


fictive_mass = 64.0
epsilon = 1e-06


def extended(cells, sides, width):
    for axis, dim in sides:
        count = lax.axis_size(axis)
        ends = count - 1
        head = lax.slice_in_dim(cells, 0, width, axis=dim)
        tail = lax.slice_in_dim(cells, cells.shape[dim] - width, cells.shape[dim], axis=dim)
        cells = jnp.concatenate(
            [
                lax.ppermute(tail, axis, [(i, (i + 1) % count) for i in range(ends)]),
                cells,
                lax.ppermute(head, axis, [((i + 1) % count, i) for i in range(ends)]),
            ],
            axis=dim,
        )
    return cells


def neighbour_table():
    table = []
    for across in range(-3, 4):
        for along in range(-3, 4):
            for upward in range(-3, 4):
                length = across * across + along * along + upward * upward
                if 0 < length <= 9:
                    table.append((across, along, upward))
    return table


def bond_forces(field_pad, words, words_pad, exist_pad):
    rows = words.shape[1]
    cols = words.shape[2]
    depth = words.shape[3]
    centre = field_pad[:, 3 : 3 + rows, 3 : 3 + cols, 3 : 3 + depth]
    totals = [jnp.zeros((rows, cols, depth), jnp.float32) for index in range(3)]
    for number, offset in enumerate(neighbour_table()):
        across, along, upward = offset
        word, bit = divmod(number, 31)
        mirror_word, mirror_bit = divmod(121 - number, 31)
        window = (
            slice(3 + across, 3 + across + rows),
            slice(3 + along, 3 + along + cols),
            slice(3 + upward, 3 + upward + depth),
        )
        other = field_pad[(slice(None),) + window]
        own_flag = words[word] >> bit & 1
        far_flag = words_pad[mirror_word][window] >> mirror_bit & 1
        intact = (own_flag | far_flag == 0) & (exist_pad[window] > 0)
        length = float(across * across + along * along + upward * upward)
        weight = 1.0 / (length * math.sqrt(length))
        stretch = (
            float(across) * (other[0] - centre[0])
            + float(along) * (other[1] - centre[1])
            + float(upward) * (other[2] - centre[2])
        )
        scaled = jnp.where(intact, stretch * weight, jnp.float32(0.0))
        totals[0] = totals[0] + float(across) * scaled
        totals[1] = totals[1] + float(along) * scaled
        totals[2] = totals[2] + float(upward) * scaled
    return jnp.stack(totals)


def depth_pad(field):
    return jnp.pad(field, ((0, 0), (0, 0), (0, 0), (3, 3)))


def on_device(disp, vel, load, flags, mask_bits):
    rows = disp.shape[1]
    cols = disp.shape[2]
    depth = disp.shape[3]
    size_x = lax.axis_size("gx")
    size_y = lax.axis_size("gy")
    count = 3.0 * rows * size_x * cols * size_y * depth
    words_rim = extended(mask_bits, (("gx", 1), ("gy", 2)), 3)
    words_pad = depth_pad(words_rim)
    places_x = lax.axis_index("gx") * rows - 3 + jnp.arange(rows + 6, dtype=jnp.int32)
    places_y = lax.axis_index("gy") * cols - 3 + jnp.arange(cols + 6, dtype=jnp.int32)
    places_z = jnp.arange(depth + 6, dtype=jnp.int32)
    inside_x = (places_x >= 0) & (places_x < rows * size_x)
    inside_y = (places_y >= 0) & (places_y < cols * size_y)
    inside_z = (places_z >= 3) & (places_z < depth + 3)
    exist_pad = (
        inside_x[:, None, None] & inside_y[None, :, None] & inside_z[None, None, :]
    ).astype(jnp.int32)
    applied = flags.astype(jnp.float32)[None] * load

    def internal(field):
        field_rim = extended(field, (("gx", 1), ("gy", 2)), 3)
        return bond_forces(depth_pad(field_rim), mask_bits, words_pad, exist_pad)

    previous = internal(disp - vel)
    field = disp
    speed = vel
    for step in range(ITERS):
        current = internal(field)
        total = current + applied
        kinetic, rayleigh = lax.psum(
            (jnp.sum(speed * speed), jnp.sum(speed * (previous - current))), ("gx", "gy")
        )
        damping = 2.0 * jnp.sqrt(rayleigh / count / (fictive_mass * (kinetic / count + epsilon)))
        alpha = (2.0 - damping) / (2.0 + damping)
        beta = 2.0 / (fictive_mass * (2.0 + damping))
        alpha, beta = (alpha, beta)
        speed = alpha * speed + beta * total
        field = field + speed
        previous = current
    return (field, speed)


def solution(mesh):
    placed = (
        P(None, "gx", "gy", None),
        P(None, "gx", "gy", None),
        P(None, "gx", "gy", None),
        P("gx", "gy", None),
        P(None, "gx", "gy", None),
    )
    return jax.shard_map(
        on_device,
        mesh=mesh,
        in_specs=placed,
        out_specs=(P(None, "gx", "gy", None), P(None, "gx", "gy", None)),
        check_vma=False,
    )
```

profile of v0, /device:TPU:0, one launch (start us, length us, event | category | flops | bytes accessed | tf_op | source)
XLA Modules:
  0.0 608.1 jit_solution(17983634218505052696)
XLA Ops:
  5.0 4.5 collective-permute-start
  13.9 4.3 collective-permute-start.4
  19.6 4.6 collective-permute-start.10
  25.6 4.9 collective-permute-start.2
  31.1 4.8 collective-permute-start.6
  44.0 8.3 %add_bitcast_fusion.23 = (f32[1,8,16,128]{3,2,1,0:T(8,128)S(1)}, f32[8,16,128]{2,1,0:T(8,128)S(1)}, pred[8,16,128]{2,1,0:T(8,128)(4,1)S(1)}, f32[8,16,128]{2,1,0...) fusion(f32[8,16,128]{2,1,0:T(8,128)S(1)} %get-tuple-element.129, ...), kind=kLoop, calls=%fused_computation.12535 | loop fusion | flops 22806528 | bytes 33044480 | tf_op jit(solution)/shard_map/stack | solution.py:73
  54.4 7.3 %add_bitcast_fusion.26 = (f32[1,8,16,128]{3,2,1,0:T(8,128)S(1)}, f32[8,16,128]{2,1,0:T(8,128)S(1)}, f32[8,16,128]{2,1,0:T(8,128)S(1)}, f32[8,16,128]{2,1,0:T(8,1...) fusion(f32[8,16,128]{2,1,0:T(8,128)S(1)} %get-tuple-element.111, ...), kind=kLoop, calls=%fused_computation.12538 | loop fusion | flops 20709376 | bytes 31277056 | tf_op jit(solution)/shard_map/stack | solution.py:73
  64.1 42.3 %all-reduce.17 = (f32[]{:T(128)}, f32[]{:T(128)}) all-reduce(f32[]{:T(128)} %get-tuple-element.17, f32[]{:T(128)} %get-tuple-element.16), channel_id=1, replica_groups=mesh['gx'=4,'gy'=8] {'gx','gy'}, use_global_device_ids=true, to_apply=%region_1.2 | all-reduce | flops 2 | bytes 16 | tf_op jit(solution)/shard_map/psum | solution.py:110
  113.2 4.2 collective-permute-start.14
  125.0 7.3 %add_bitcast_fusion.20 = (f32[1,8,16,128]{3,2,1,0:T(8,128)S(1)}, f32[8,16,128]{2,1,0:T(8,128)S(1)}, f32[8,16,128]{2,1,0:T(8,128)S(1)}, f32[8,16,128]{2,1,0:T(8,1...) fusion(f32[8,16,128]{2,1,0:T(8,128)S(1)} %get-tuple-element.127, ...), kind=kLoop, calls=%fused_computation.12532 | loop fusion | flops 20709376 | bytes 31277056 | tf_op jit(solution)/shard_map/stack | solution.py:73
  134.7 42.6 %all-reduce.16 = (f32[]{:T(128)}, f32[]{:T(128)}) all-reduce(f32[]{:T(128)} %get-tuple-element.15, f32[]{:T(128)} %get-tuple-element.14), channel_id=1, replica_groups=mesh['gx'=4,'gy'=8] {'gx','gy'}, use_global_device_ids=true, to_apply=%region_5.6 | all-reduce | flops 2 | bytes 16 | tf_op jit(solution)/shard_map/psum | solution.py:110
  185.0 4.2 collective-permute-start.18
  196.8 7.3 %add_bitcast_fusion.17 = (f32[1,8,16,128]{3,2,1,0:T(8,128)S(1)}, f32[8,16,128]{2,1,0:T(8,128)S(1)}, f32[8,16,128]{2,1,0:T(8,128)S(1)}, f32[8,16,128]{2,1,0:T(8,1...) fusion(f32[8,16,128]{2,1,0:T(8,128)S(1)} %get-tuple-element.126, ...), kind=kLoop, calls=%fused_computation.12529 | loop fusion | flops 20709376 | bytes 31277056 | tf_op jit(solution)/shard_map/stack | solution.py:73
  206.4 42.7 %all-reduce.15 = (f32[]{:T(128)}, f32[]{:T(128)}) all-reduce(f32[]{:T(128)} %get-tuple-element.13, f32[]{:T(128)} %get-tuple-element.12), channel_id=1, replica_groups=mesh['gx'=4,'gy'=8] {'gx','gy'}, use_global_device_ids=true, to_apply=%region_9.10 | all-reduce | flops 2 | bytes 16 | tf_op jit(solution)/shard_map/psum | solution.py:110
  268.6 7.3 %add_bitcast_fusion.14 = (f32[1,8,16,128]{3,2,1,0:T(8,128)S(1)}, f32[8,16,128]{2,1,0:T(8,128)S(1)}, f32[8,16,128]{2,1,0:T(8,128)S(1)}, f32[8,16,128]{2,1,0:T(8,1...) fusion(f32[8,16,128]{2,1,0:T(8,128)S(1)} %get-tuple-element.125, ...), kind=kLoop, calls=%fused_computation.12526 | loop fusion | flops 20709376 | bytes 31277056 | tf_op jit(solution)/shard_map/stack | solution.py:73
  278.2 42.6 %all-reduce.14 = (f32[]{:T(128)}, f32[]{:T(128)}) all-reduce(f32[]{:T(128)} %get-tuple-element.11, f32[]{:T(128)} %get-tuple-element.10), channel_id=1, replica_groups=mesh['gx'=4,'gy'=8] {'gx','gy'}, use_global_device_ids=true, to_apply=%region_13.14 | all-reduce | flops 2 | bytes 16 | tf_op jit(solution)/shard_map/psum | solution.py:110
  339.5 7.3 %add_bitcast_fusion.11 = (f32[1,8,16,128]{3,2,1,0:T(8,128)S(1)}, f32[8,16,128]{2,1,0:T(8,128)S(1)}, f32[8,16,128]{2,1,0:T(8,128)S(1)}, f32[8,16,128]{2,1,0:T(8,1...) fusion(f32[8,16,128]{2,1,0:T(8,128)S(1)} %get-tuple-element.124, ...), kind=kLoop, calls=%fused_computation.12523 | loop fusion | flops 20709376 | bytes 31277056 | tf_op jit(solution)/shard_map/stack | solution.py:73
  349.2 42.6 %all-reduce.13 = (f32[]{:T(128)}, f32[]{:T(128)}) all-reduce(f32[]{:T(128)} %get-tuple-element.9, f32[]{:T(128)} %get-tuple-element.8), channel_id=1, replica_groups=mesh['gx'=4,'gy'=8] {'gx','gy'}, use_global_device_ids=true, to_apply=%region_17.18 | all-reduce | flops 2 | bytes 16 | tf_op jit(solution)/shard_map/psum | solution.py:110
  411.3 7.3 %add_bitcast_fusion.8 = (f32[1,8,16,128]{3,2,1,0:T(8,128)S(1)}, f32[8,16,128]{2,1,0:T(8,128)S(1)}, f32[8,16,128]{2,1,0:T(8,128)S(1)}, f32[8,16,128]{2,1,0:T(8,12...) fusion(f32[8,16,128]{2,1,0:T(8,128)S(1)} %get-tuple-element.123, ...), kind=kLoop, calls=%fused_computation.12520 | loop fusion | flops 20709376 | bytes 31277056 | tf_op jit(solution)/shard_map/stack | solution.py:73
  420.9 42.7 %all-reduce.12 = (f32[]{:T(128)}, f32[]{:T(128)}) all-reduce(f32[]{:T(128)} %get-tuple-element.7, f32[]{:T(128)} %get-tuple-element.6), channel_id=1, replica_groups=mesh['gx'=4,'gy'=8] {'gx','gy'}, use_global_device_ids=true, to_apply=%region_21.22 | all-reduce | flops 2 | bytes 16 | tf_op jit(solution)/shard_map/psum | solution.py:110
  482.2 7.3 %add_bitcast_fusion.5 = (f32[1,8,16,128]{3,2,1,0:T(8,128)S(1)}, f32[8,16,128]{2,1,0:T(8,128)S(1)}, f32[8,16,128]{2,1,0:T(8,128)S(1)}, f32[8,16,128]{2,1,0:T(8,12...) fusion(f32[8,16,128]{2,1,0:T(8,128)S(1)} %get-tuple-element.122, ...), kind=kLoop, calls=%fused_computation.12517 | loop fusion | flops 20709376 | bytes 31277056 | tf_op jit(solution)/shard_map/stack | solution.py:73
  491.8 42.6 %all-reduce.11 = (f32[]{:T(128)}, f32[]{:T(128)}) all-reduce(f32[]{:T(128)} %get-tuple-element.5, f32[]{:T(128)} %get-tuple-element.4), channel_id=1, replica_groups=mesh['gx'=4,'gy'=8] {'gx','gy'}, use_global_device_ids=true, to_apply=%region_25.26 | all-reduce | flops 2 | bytes 16 | tf_op jit(solution)/shard_map/psum | solution.py:110
  553.0 7.3 %add_bitcast_fusion.2 = (f32[1,8,16,128]{3,2,1,0:T(8,128)S(1)}, f32[8,16,128]{2,1,0:T(8,128)S(1)}, f32[8,16,128]{2,1,0:T(8,128)S(1)}, f32[8,16,128]{2,1,0:T(8,12...) fusion(f32[8,16,128]{2,1,0:T(8,128)S(1)} %get-tuple-element.121, ...), kind=kLoop, calls=%fused_computation.12514 | loop fusion | flops 20709376 | bytes 31277056 | tf_op jit(solution)/shard_map/stack | solution.py:73
  562.7 42.6 %all-reduce.10 = (f32[]{:T(128)}, f32[]{:T(128)}) all-reduce(f32[]{:T(128)} %get-tuple-element.3, f32[]{:T(128)} %get-tuple-element.2), channel_id=1, replica_groups=mesh['gx'=4,'gy'=8] {'gx','gy'}, use_global_device_ids=true, to_apply=%region_29.30 | all-reduce | flops 2 | bytes 16 | tf_op jit(solution)/shard_map/psum | solution.py:110
  (257 shorter events, 155.0 us)
Async XLA Ops:
  1.7 10.8 %collective-permute-start.8 = (f32[3,3,16,128]{3,2,1,0:T(8,128)S(1)}, f32[3,3,16,128]{3,2,1,0:T(8,128)S(1)}, u32[]{:S(2)}, u32[]{:S(2)}) collective-permute-start(f32[3,3,16,128]{3,2,1,0:T(8,128)S(1)} %get-tuple-element.1356), channel_id=1, source_target_pairs={{0,8},{8,16},{16,24},{1,9},{9,17},{17,25},{2,10},{10,18},{18,26},{... | collective-permute-start | bytes 221192 | tf_op jit(solution)/shard_map/ppermute | solution.py:23
  5.0 14.5 %collective-permute-start = (s32[4,3,16,128]{3,2,1,0:T(8,128)S(1)}, s32[4,3,16,128]{3,2,1,0:T(8,128)S(1)}, u32[]{:S(2)}, u32[]{:S(2)}) collective-permute-start(s32[4,3,16,128]{3,2,1,0:T(8,128)S(1)} %get-tuple-element.1336), channel_id=1, source_target_pairs={{0,8},{8,16},{16,24},{1,9},{9,17},{17,25},{2,10},{10,18},{18,26},{... | collective-permute-start | bytes 294920 | tf_op jit(solution)/shard_map/ppermute | solution.py:23
  9.6 14.6 %collective-permute-start.1 = (s32[4,3,16,128]{3,2,1,0:T(8,128)S(1)}, s32[4,3,16,128]{3,2,1,0:T(8,128)S(1)}, u32[]{:S(2)}, u32[]{:S(2)}) collective-permute-start(s32[4,3,16,128]{3,2,1,0:T(8,128)S(1)} %get-tuple-element.1335), channel_id=1, source_target_pairs={{8,0},{16,8},{24,16},{9,1},{17,9},{25,17},{10,2},{18,10},{26,18},{... | collective-permute-start | bytes 294920 | tf_op jit(solution)/shard_map/ppermute | solution.py:25
  10.9 7.3 %collective-permute-start.9 = (f32[3,3,16,128]{3,2,1,0:T(8,128)S(1)}, f32[3,3,16,128]{3,2,1,0:T(8,128)S(1)}, u32[]{:S(2)}, u32[]{:S(2)}) collective-permute-start(f32[3,3,16,128]{3,2,1,0:T(8,128)S(1)} %get-tuple-element.1355), channel_id=1, source_target_pairs={{8,0},{16,8},{24,16},{9,1},{17,9},{25,17},{10,2},{18,10},{26,18},{... | collective-permute-start | bytes 221192 | tf_op jit(solution)/shard_map/ppermute | solution.py:25
  12.6 18.5 %collective-permute-start.5 = (f32[3,3,16,128]{3,2,1,0:T(8,128)S(1)}, f32[3,3,16,128]{3,2,1,0:T(8,128)S(1)}, u32[]{:S(2)}, u32[]{:S(2)}) collective-permute-start(f32[3,3,16,128]{3,2,1,0:T(8,128)S(1)} %get-tuple-element.1358), channel_id=1, source_target_pairs={{8,0},{16,8},{24,16},{9,1},{17,9},{25,17},{10,2},{18,10},{26,18},{... | collective-permute-start | bytes 221192 | tf_op jit(solution)/shard_map/ppermute | solution.py:25
  13.9 17.2 %collective-permute-start.4 = (f32[3,3,16,128]{3,2,1,0:T(8,128)S(1)}, f32[3,3,16,128]{3,2,1,0:T(8,128)S(1)}, u32[]{:S(2)}, u32[]{:S(2)}) collective-permute-start(f32[3,3,16,128]{3,2,1,0:T(8,128)S(1)} %get-tuple-element.1357), channel_id=1, source_target_pairs={{0,8},{8,16},{16,24},{1,9},{9,17},{17,25},{2,10},{10,18},{18,26},{... | collective-permute-start | bytes 221192 | tf_op jit(solution)/shard_map/ppermute | solution.py:23
  18.3 7.3 %collective-permute-start.11 = (f32[3,14,3,128]{3,2,1,0:T(4,128)S(1)}, f32[3,14,3,128]{3,2,1,0:T(4,128)S(1)}, u32[]{:S(2)}, u32[]{:S(2)}) collective-permute-start(f32[3,14,3,128]{3,2,1,0:T(4,128)S(1)} %get-tuple-element.1330), channel_id=1, source_target_pairs={{1,0},{2,1},{3,2},{4,3},{5,4},{6,5},{7,6},{9,8},{10,9},{11,10},{12... | collective-permute-start | bytes 193544 | tf_op jit(solution)/shard_map/ppermute | solution.py:25
  19.6 10.9 %collective-permute-start.10 = (f32[3,14,3,128]{3,2,1,0:T(4,128)S(1)}, f32[3,14,3,128]{3,2,1,0:T(4,128)S(1)}, u32[]{:S(2)}, u32[]{:S(2)}) collective-permute-start(f32[3,14,3,128]{3,2,1,0:T(4,128)S(1)} %get-tuple-element.1329), channel_id=1, source_target_pairs={{0,1},{1,2},{2,3},{3,4},{4,5},{5,6},{6,7},{8,9},{9,10},{10,11},{11... | collective-permute-start | bytes 193544 | tf_op jit(solution)/shard_map/ppermute | solution.py:23
  24.3 13.0 %collective-permute-start.3 = (s32[4,14,3,128]{3,2,1,0:T(4,128)S(1)}, s32[4,14,3,128]{3,2,1,0:T(4,128)S(1)}, u32[]{:S(2)}, u32[]{:S(2)}) collective-permute-start(s32[4,14,3,128]{3,2,1,0:T(4,128)S(1)} %get-tuple-element.1300), channel_id=1, source_target_pairs={{1,0},{2,1},{3,2},{4,3},{5,4},{6,5},{7,6},{9,8},{10,9},{11,10},{12... | collective-permute-start | bytes 258056 | tf_op jit(solution)/shard_map/ppermute | solution.py:25
  25.6 11.7 %collective-permute-start.2 = (s32[4,14,3,128]{3,2,1,0:T(4,128)S(1)}, s32[4,14,3,128]{3,2,1,0:T(4,128)S(1)}, u32[]{:S(2)}, u32[]{:S(2)}) collective-permute-start(s32[4,14,3,128]{3,2,1,0:T(4,128)S(1)} %get-tuple-element.1299), channel_id=1, source_target_pairs={{0,1},{1,2},{2,3},{3,4},{4,5},{5,6},{6,7},{8,9},{9,10},{10,11},{11... | collective-permute-start | bytes 258056 | tf_op jit(solution)/shard_map/ppermute | solution.py:23
  31.1 11.2 %collective-permute-start.6 = (f32[3,14,3,128]{3,2,1,0:T(4,128)S(1)}, f32[3,14,3,128]{3,2,1,0:T(4,128)S(1)}, u32[]{:S(2)}, u32[]{:S(2)}) collective-permute-start(f32[3,14,3,128]{3,2,1,0:T(4,128)S(1)} %get-tuple-element.1333), channel_id=1, source_target_pairs={{0,1},{1,2},{2,3},{3,4},{4,5},{5,6},{6,7},{8,9},{9,10},{10,11},{11... | collective-permute-start | bytes 193544 | tf_op jit(solution)/shard_map/ppermute | solution.py:23
  35.9 6.7 %collective-permute-start.7 = (f32[3,14,3,128]{3,2,1,0:T(4,128)S(1)}, f32[3,14,3,128]{3,2,1,0:T(4,128)S(1)}, u32[]{:S(2)}, u32[]{:S(2)}) collective-permute-start(f32[3,14,3,128]{3,2,1,0:T(4,128)S(1)} %get-tuple-element.1334), channel_id=1, source_target_pairs={{1,0},{2,1},{3,2},{4,3},{5,4},{6,5},{7,6},{9,8},{10,9},{11,10},{12... | collective-permute-start | bytes 193544 | tf_op jit(solution)/shard_map/ppermute | solution.py:25
  113.2 6.6 %collective-permute-start.14 = (f32[3,14,3,128]{3,2,1,0:T(4,128)S(1)}, f32[3,14,3,128]{3,2,1,0:T(4,128)S(1)}, u32[]{:S(2)}, u32[]{:S(2)}) collective-permute-start(f32[3,14,3,128]{3,2,1,0:T(4,128)S(1)} %get-tuple-element.1327), channel_id=1, source_target_pairs={{0,1},{1,2},{2,3},{3,4},{4,5},{5,6},{6,7},{8,9},{9,10},{10,11},{11... | collective-permute-start | bytes 193544 | tf_op jit(solution)/shard_map/ppermute | solution.py:23
  117.4 6.6 %collective-permute-start.15 = (f32[3,14,3,128]{3,2,1,0:T(4,128)S(1)}, f32[3,14,3,128]{3,2,1,0:T(4,128)S(1)}, u32[]{:S(2)}, u32[]{:S(2)}) collective-permute-start(f32[3,14,3,128]{3,2,1,0:T(4,128)S(1)} %get-tuple-element.1328), channel_id=1, source_target_pairs={{1,0},{2,1},{3,2},{4,3},{5,4},{6,5},{7,6},{9,8},{10,9},{11,10},{12... | collective-permute-start | bytes 193544 | tf_op jit(solution)/shard_map/ppermute | solution.py:25
  185.0 6.6 %collective-permute-start.18 = (f32[3,14,3,128]{3,2,1,0:T(4,128)S(1)}, f32[3,14,3,128]{3,2,1,0:T(4,128)S(1)}, u32[]{:S(2)}, u32[]{:S(2)}) collective-permute-start(f32[3,14,3,128]{3,2,1,0:T(4,128)S(1)} %get-tuple-element.1323), channel_id=1, source_target_pairs={{0,1},{1,2},{2,3},{3,4},{4,5},{5,6},{6,7},{8,9},{9,10},{10,11},{11... | collective-permute-start | bytes 193544 | tf_op jit(solution)/shard_map/ppermute | solution.py:23
  189.2 6.6 %collective-permute-start.19 = (f32[3,14,3,128]{3,2,1,0:T(4,128)S(1)}, f32[3,14,3,128]{3,2,1,0:T(4,128)S(1)}, u32[]{:S(2)}, u32[]{:S(2)}) collective-permute-start(f32[3,14,3,128]{3,2,1,0:T(4,128)S(1)} %get-tuple-element.1324), channel_id=1, source_target_pairs={{1,0},{2,1},{3,2},{4,3},{5,4},{6,5},{7,6},{9,8},{10,9},{11,10},{12... | collective-permute-start | bytes 193544 | tf_op jit(solution)/shard_map/ppermute | solution.py:25
  256.8 6.6 %collective-permute-start.22 = (f32[3,14,3,128]{3,2,1,0:T(4,128)S(1)}, f32[3,14,3,128]{3,2,1,0:T(4,128)S(1)}, u32[]{:S(2)}, u32[]{:S(2)}) collective-permute-start(f32[3,14,3,128]{3,2,1,0:T(4,128)S(1)} %get-tuple-element.1319), channel_id=1, source_target_pairs={{0,1},{1,2},{2,3},{3,4},{4,5},{5,6},{6,7},{8,9},{9,10},{10,11},{11... | collective-permute-start | bytes 193544 | tf_op jit(solution)/shard_map/ppermute | solution.py:23
  261.0 6.6 %collective-permute-start.23 = (f32[3,14,3,128]{3,2,1,0:T(4,128)S(1)}, f32[3,14,3,128]{3,2,1,0:T(4,128)S(1)}, u32[]{:S(2)}, u32[]{:S(2)}) collective-permute-start(f32[3,14,3,128]{3,2,1,0:T(4,128)S(1)} %get-tuple-element.1320), channel_id=1, source_target_pairs={{1,0},{2,1},{3,2},{4,3},{5,4},{6,5},{7,6},{9,8},{10,9},{11,10},{12... | collective-permute-start | bytes 193544 | tf_op jit(solution)/shard_map/ppermute | solution.py:25
  327.7 6.6 %collective-permute-start.26 = (f32[3,14,3,128]{3,2,1,0:T(4,128)S(1)}, f32[3,14,3,128]{3,2,1,0:T(4,128)S(1)}, u32[]{:S(2)}, u32[]{:S(2)}) collective-permute-start(f32[3,14,3,128]{3,2,1,0:T(4,128)S(1)} %get-tuple-element.1315), channel_id=1, source_target_pairs={{0,1},{1,2},{2,3},{3,4},{4,5},{5,6},{6,7},{8,9},{9,10},{10,11},{11... | collective-permute-start | bytes 193544 | tf_op jit(solution)/shard_map/ppermute | solution.py:23
  331.9 6.6 %collective-permute-start.27 = (f32[3,14,3,128]{3,2,1,0:T(4,128)S(1)}, f32[3,14,3,128]{3,2,1,0:T(4,128)S(1)}, u32[]{:S(2)}, u32[]{:S(2)}) collective-permute-start(f32[3,14,3,128]{3,2,1,0:T(4,128)S(1)} %get-tuple-element.1316), channel_id=1, source_target_pairs={{1,0},{2,1},{3,2},{4,3},{5,4},{6,5},{7,6},{9,8},{10,9},{11,10},{12... | collective-permute-start | bytes 193544 | tf_op jit(solution)/shard_map/ppermute | solution.py:25
  399.5 6.6 %collective-permute-start.30 = (f32[3,14,3,128]{3,2,1,0:T(4,128)S(1)}, f32[3,14,3,128]{3,2,1,0:T(4,128)S(1)}, u32[]{:S(2)}, u32[]{:S(2)}) collective-permute-start(f32[3,14,3,128]{3,2,1,0:T(4,128)S(1)} %get-tuple-element.1311), channel_id=1, source_target_pairs={{0,1},{1,2},{2,3},{3,4},{4,5},{5,6},{6,7},{8,9},{9,10},{10,11},{11... | collective-permute-start | bytes 193544 | tf_op jit(solution)/shard_map/ppermute | solution.py:23
  403.7 6.6 %collective-permute-start.31 = (f32[3,14,3,128]{3,2,1,0:T(4,128)S(1)}, f32[3,14,3,128]{3,2,1,0:T(4,128)S(1)}, u32[]{:S(2)}, u32[]{:S(2)}) collective-permute-start(f32[3,14,3,128]{3,2,1,0:T(4,128)S(1)} %get-tuple-element.1312), channel_id=1, source_target_pairs={{1,0},{2,1},{3,2},{4,3},{5,4},{6,5},{7,6},{9,8},{10,9},{11,10},{12... | collective-permute-start | bytes 193544 | tf_op jit(solution)/shard_map/ppermute | solution.py:25
  470.4 6.6 %collective-permute-start.34 = (f32[3,14,3,128]{3,2,1,0:T(4,128)S(1)}, f32[3,14,3,128]{3,2,1,0:T(4,128)S(1)}, u32[]{:S(2)}, u32[]{:S(2)}) collective-permute-start(f32[3,14,3,128]{3,2,1,0:T(4,128)S(1)} %get-tuple-element.1307), channel_id=1, source_target_pairs={{0,1},{1,2},{2,3},{3,4},{4,5},{5,6},{6,7},{8,9},{9,10},{10,11},{11... | collective-permute-start | bytes 193544 | tf_op jit(solution)/shard_map/ppermute | solution.py:23
  541.3 6.6 %collective-permute-start.38 = (f32[3,14,3,128]{3,2,1,0:T(4,128)S(1)}, f32[3,14,3,128]{3,2,1,0:T(4,128)S(1)}, u32[]{:S(2)}, u32[]{:S(2)}) collective-permute-start(f32[3,14,3,128]{3,2,1,0:T(4,128)S(1)} %get-tuple-element.1303), channel_id=1, source_target_pairs={{0,1},{1,2},{2,3},{3,4},{4,5},{5,6},{6,7},{8,9},{9,10},{10,11},{11... | collective-permute-start | bytes 193544 | tf_op jit(solution)/shard_map/ppermute | solution.py:23
  (35 other events, 351.5 us)
where the time goes:
time: 620 us; the launch traced here: 608 us
  blocking collectives  341 us (55%)
  other arithmetic  105 us (17%)
  starting transfers between devices  103 us (17%)
  waiting for transfers between devices  42.6 us (7%)
  between operations  14.4 us (2%)
    psum x8, blocking collectives, on_device(): lax.psum((jnp.sum(speed * speed), jnp.sum(speed * (previous - current))),...  341 us
    another operation x27, other arithmetic, bond_forces(): return jnp.stack(totals)  81.3 us
    ppermute x20, starting transfers between devices, extended(): lax.ppermute(tail, axis, [(i, (i + 1) % count) for i in range(ends)])  76.1 us
    ppermute x20, waiting for transfers between devices, extended(): lax.ppermute(head, axis, [((i + 1) % count, i) for i in range(ends)])  29.2 us
    ppermute x20, starting transfers between devices, extended(): lax.ppermute(head, axis, [((i + 1) % count, i) for i in range(ends)])  26.6 us
    ppermute x20, waiting for transfers between devices, extended(): lax.ppermute(tail, axis, [(i, (i + 1) % count) for i in range(ends)])  13.4 us
  transfers between devices with their start and end apart: 40, of which 22 were waited for; matrix products, arithmetic and copies ran while one was open for 1% of the time, Pallas kernels for 0%

commit v1 on v0

v1 whole, which is shorter than its diff:
```python
import functools
import math

import jax
import jax.numpy as jnp
from jax import lax
from jax.experimental import pallas as pl
from jax.experimental.pallas import tpu as pltpu
from jax.sharding import PartitionSpec as P

ITERS = 8
MESH = pl.DeviceIdType.MESH

fictive_mass = 64.0
epsilon = 1e-06

EDGE = 8


def neighbour_table():
    table = []
    for across in range(-3, 4):
        for along in range(-3, 4):
            for upward in range(-3, 4):
                length = across * across + along * along + upward * upward
                if 0 < length <= 9:
                    table.append((across, along, upward))
    return table


TABLE = neighbour_table()
NUMBER = {offset: number for number, offset in enumerate(TABLE)}


def reach(along, upward):
    return [a for a in range(-3, 4) if (a, along, upward) in NUMBER]


def rolled(cells, upward):
    depth = cells.shape[-1]
    if upward == 0:
        return cells
    return pltpu.roll(cells, (-upward) % depth, cells.ndim - 1)


def kernel(
    nx, ny,
    disp, vel, load, flags, mask,
    field, speed,
    weights, diagonal, pad, mask_pad, shifted, mask_shifted, mixed, plain, force, total, change,
    rim_x, rim_y, rim_c, pack_y, pack_c,
    mrim_x, mrim_y, mrim_c, mpack_y, mpack_c,
    sums_out, sums_in,
    send_sem, recv_sem, msend_sem, mrecv_sem, sum_send_sem, sum_recv_sem,
):
    rows, cols, depth = flags.shape
    count = 3.0 * rows * nx * cols * ny * depth
    devices = nx * ny
    my_x = lax.axis_index("gx")
    my_y = lax.axis_index("gy")

    sides = []
    for step_x, step_y in ((-1, 0), (1, 0), (0, -1), (0, 1), (-1, -1), (-1, 1), (1, -1), (1, 1)):
        there = None
        for step, mine, size in ((step_x, my_x, nx), (step_y, my_y, ny)):
            if step:
                near = mine > 0 if step < 0 else mine < size - 1
                there = near if there is None else there & near
        sides.append((step_x, step_y, there))

    def copies(index, source, rims, packs, sems, slot):
        step_x, step_y, there = sides[index]
        target = (my_x + step_x, my_y + step_y)
        if index < 2:
            start = 0 if step_x < 0 else rows - 3
            src = source.at[:, pl.ds(start, 3)]
            dst = rims[0].at[slot, 1 - index]
        elif index < 4:
            src = packs[0].at[slot, index - 2]
            dst = rims[1].at[slot, 3 - index]
        else:
            src = packs[1].at[slot, index - 4]
            dst = rims[2].at[slot, 7 - index]
        return pltpu.make_async_remote_copy(
            src_ref=src, dst_ref=dst,
            send_sem=sems[0].at[slot, index], recv_sem=sems[1].at[slot, index ^ 1 if index < 4 else 11 - index],
            device_id=target, device_id_type=MESH,
        )

    def exchange(source, rims, packs, sems, slot):
        for index in (0, 1):
            @pl.when(sides[index][2])
            def _():
                copies(index, source, rims, packs, sems, slot).start()
        parts = source.shape[0]
        for c in range(parts):
            for j in range(3):
                packs[0][slot, 0, c, j] = source[c, :, j, :]
                packs[0][slot, 1, c, j] = source[c, :, cols - 3 + j, :]
            for corner in range(4):
                step_x, step_y, _ = sides[4 + corner]
                for i in range(2):
                    x = i if step_x < 0 else rows - 2 + i
                    y = 0 if step_y < 0 else cols - 2
                    packs[1][slot, corner, c, pl.ds(2 * i, 2), :] = source[c, x, pl.ds(y, 2), :]
        for index in range(2, 8):
            @pl.when(sides[index][2])
            def _():
                copies(index, source, rims, packs, sems, slot).start()

    def arrive(source, rims, packs, sems, slot, padded):
        parts = source.shape[0]
        for index in range(8):
            step_x, step_y, there = sides[index]

            @pl.when(there)
            def _():
                step = copies(index, source, rims, packs, sems, slot)
                step.wait_send()
                back = copies(index ^ 1 if index < 4 else 11 - index, source, rims, packs, sems, slot)
                back.wait_recv()
                if index < 2:
                    first = 0 if step_x < 0 else 3 + rows
                    padded[:, pl.ds(first, 3), pl.ds(EDGE, cols), :] = rims[0][slot, index]
                elif index < 4:
                    first = EDGE - 3 if step_y < 0 else EDGE + cols
                    for c in range(parts):
                        for j in range(3):
                            padded[c, pl.ds(3, rows), first + j, :] = rims[1][slot, index - 2, c, j]
                else:
                    x = 1 if step_x < 0 else 3 + rows
                    y = EDGE - 2 if step_y < 0 else EDGE + cols
                    for c in range(parts):
                        for i in range(2):
                            padded[c, x + i, pl.ds(y, 2), :] = rims[2][slot, index - 4, c, pl.ds(2 * i, 2), :]

    rims, packs, sems = (rim_x, rim_y, rim_c), (pack_y, pack_c), (send_sem, recv_sem)
    mrims, mpacks, msems = (mrim_x, mrim_y, mrim_c), (mpack_y, mpack_c), (msend_sem, mrecv_sem)

    exchange(mask, mrims, mpacks, msems, 0)
    exchange(vel, rims, packs, sems, 0)
    exchange(disp, rims, packs, sems, 1)

    pad[...] = jnp.zeros_like(pad)
    mask_pad[...] = jnp.full_like(mask_pad, -1)
    mask_pad[:, pl.ds(3, rows), pl.ds(EDGE, cols), :] = mask[...]
    field[...] = disp[...]
    speed[...] = vel[...]
    diagonal[...] = jnp.zeros_like(diagonal)
    arrive(mask, mrims, mpacks, msems, 0, mask_pad)

    place = lax.broadcasted_iota(jnp.int32, (1, 1, depth), 2)
    for along in range(-3, 4):
        for word in range(4):
            mask_shifted[word] = mask_pad[word, :, pl.ds(EDGE + along, cols), :]
        for upward in range(-3, 4):
            across_all = reach(along, upward)
            if not across_all:
                continue
            inside = (place + upward >= 0) & (place + upward < depth)
            for low in range(0, rows, 4):
                moments = [None, None, None]
                for across in across_all:
                    number = NUMBER[(across, along, upward)]
                    word, bit = divmod(number, 31)
                    mirror_word, mirror_bit = divmod(121 - number, 31)
                    length = float(across * across + along * along + upward * upward)
                    weight = 1.0 / (length * math.sqrt(length))
                    own = mask[word, pl.ds(low, 4)] & (1 << bit)
                    far = mask_shifted[mirror_word, pl.ds(3 + low + across, 4)] & (1 << mirror_bit)
                    far = rolled(jnp.where(far == 0, jnp.float32(weight), jnp.float32(0.0)), upward)
                    one = jnp.where((own == 0) & inside, far, jnp.float32(0.0))
                    weights[number, pl.ds(low, 4)] = one
                    for power in range(3):
                        scale = float(across**power)
                        if scale != 0.0:
                            term = one if scale == 1.0 else scale * one
                            moments[power] = term if moments[power] is None else moments[power] + term
                for slot, (power, scale) in enumerate((
                    (2, 1), (1, along), (1, upward), (0, along * along), (0, along * upward), (0, upward * upward),
                )):
                    if scale and moments[power] is not None:
                        diagonal[slot, pl.ds(low, 4)] += float(scale) * moments[power]

    def apply_forces():
        for low in range(0, rows, 4):
            here = pl.ds(low, 4)
            u = [pad[c, pl.ds(3 + low, 4), pl.ds(EDGE, cols), :] for c in range(3)]
            d = [diagonal[slot, here] for slot in range(6)]
            force[0, here] = -(d[0] * u[0] + d[1] * u[1] + d[2] * u[2])
            force[1, here] = -(d[1] * u[0] + d[3] * u[1] + d[4] * u[2])
            force[2, here] = -(d[2] * u[0] + d[4] * u[1] + d[5] * u[2])
        turn = 0
        for along in range(-3, 4):
            for c in range(3):
                shifted[c] = pad[c, :, pl.ds(EDGE + along, cols), :]
            for upward in range(-3, 4):
                across_all = reach(along, upward)
                if not across_all:
                    continue
                turn = 1 - turn
                most = max(across_all)
                span = pl.ds(3 - most, rows + 2 * most)
                if along or upward:
                    mix = None
                    for scale, c in ((along, 1), (upward, 2)):
                        if scale:
                            term = float(scale) * shifted[c, span] if scale != 1 else shifted[c, span]
                            mix = term if mix is None else mix + term
                    mixed[turn, span] = rolled(mix, upward)
                if most:
                    plain[turn, span] = rolled(shifted[0, span], upward)
                for low in range(0, rows, 4):
                    here = pl.ds(low, 4)
                    whole = None
                    lean = None

                    def stretch(across):
                        at = pl.ds(3 + low + across, 4)
                        value = mixed[turn, at] if along or upward else None
                        if across:
                            term = float(across) * plain[turn, at]
                            value = term if value is None else value + term
                        return weights[NUMBER[(across, along, upward)], here] * value

                    for across in [a for a in across_all if a >= 0]:
                        if across == 0:
                            whole = stretch(0)
                            continue
                        up, down = stretch(across), stretch(-across)
                        both = up + down
                        whole = both if whole is None else whole + both
                        gap = float(across) * (up - down) if across != 1 else up - down
                        lean = gap if lean is None else lean + gap
                    if lean is not None:
                        force[0, here] += lean
                    if along:
                        force[1, here] += float(along) * whole
                    if upward:
                        force[2, here] += float(upward) * whole

    me = my_x * ny + my_y

    def send_sums(slot):
        kinetic = jnp.sum(speed[...] * speed[...], axis=(0, 1))
        rayleigh = jnp.sum(speed[...] * change[...], axis=(0, 1))
        sums_out[slot, pl.ds(0, 1), :] = jnp.sum(kinetic, axis=0, keepdims=True)
        sums_out[slot, pl.ds(1, 1), :] = jnp.sum(rayleigh, axis=0, keepdims=True)

        def send(r, carry):
            target = lax.rem(me + 1 + r, devices)
            pltpu.make_async_remote_copy(
                src_ref=sums_out.at[slot], dst_ref=sums_in.at[slot, r],
                send_sem=sum_send_sem.at[slot], recv_sem=sum_recv_sem.at[slot],
                device_id=(target // ny, lax.rem(target, ny)), device_id_type=MESH,
            ).start()
            return carry

        lax.fori_loop(0, devices - 1, send, 0)

    def take_sums(slot):
        whole = sums_in.at[slot]
        pltpu.make_async_copy(whole, whole, sum_send_sem.at[slot]).wait()
        pltpu.make_async_copy(whole, whole, sum_recv_sem.at[slot]).wait()
        both = jnp.sum(sums_in[slot], axis=0) + sums_out[slot]
        both = jnp.sum(both, axis=1, keepdims=True)
        kinetic = both[0:1]
        rayleigh = -both[1:2]
        damping = 2.0 * jnp.sqrt(rayleigh / count / (fictive_mass * (kinetic / count + epsilon)))
        alpha = (2.0 - damping) / (2.0 + damping)
        beta = 2.0 / (fictive_mass * (2.0 + damping))
        return alpha[None, None], beta[None, None]

    def advance(alpha, beta):
        for c in range(3):
            speed[c] = alpha[0] * speed[c] + beta[0] * total[c]
            field[c] = field[c] + speed[c]

    middle = (slice(None), pl.ds(3, rows), pl.ds(EDGE, cols), slice(None))

    def step(turn, carry):
        slot = jnp.where(turn < 2, turn, 2 + lax.rem(turn, 2))

        @pl.when(turn == 0)
        def _():
            pad[middle] = vel[...]

        @pl.when(turn == 1)
        def _():
            pad[middle] = disp[...]

        @pl.when(turn >= 2)
        def _():
            pad[middle] = total[...]

        arrive(total, rims, packs, sems, slot, pad)
        apply_forces()

        @pl.when(turn == 0)
        def _():
            change[...] = force[...]
            send_sums(0)

        @pl.when(turn == 1)
        def _():
            for c in range(3):
                total[c] = force[c] + flags[...].astype(jnp.float32) * load[c]
            exchange(total, rims, packs, sems, 2)

        @pl.when(turn >= 2)
        def _():
            alpha, beta = take_sums(lax.rem(turn, 2))
            advance(alpha, beta)
            for c in range(3):
                change[c] = alpha[0] * change[c] + beta[0] * force[c]
                total[c] = total[c] + change[c]

            @pl.when(turn < ITERS)
            def _():
                exchange(total, rims, packs, sems, 2 + lax.rem(turn + 1, 2))

            send_sums(lax.rem(turn + 1, 2))

        return carry

    lax.fori_loop(0, ITERS + 1, step, 0)
    alpha, beta = take_sums((ITERS + 1) % 2)
    advance(alpha, beta)


def on_device(nx, ny, disp, vel, load, flags, mask_bits):
    parts, rows, cols, depth = disp.shape
    words = mask_bits.shape[0]
    f32, i32 = jnp.float32, jnp.int32
    vmem, dma = pltpu.VMEM, pltpu.SemaphoreType.DMA
    wide = cols + 2 * EDGE
    block = (parts, rows, cols, depth)
    scratch = [
        vmem((len(TABLE), rows, cols, depth), f32),
        vmem((6, rows, cols, depth), f32),
        vmem((parts, rows + 6, wide, depth), f32),
        vmem((words, rows + 6, wide, depth), i32),
        vmem((parts, rows + 6, cols, depth), f32),
        vmem((words, rows + 6, cols, depth), i32),
        vmem((2, rows + 6, cols, depth), f32),
        vmem((2, rows + 6, cols, depth), f32),
        vmem(block, f32),
        vmem(block, f32),
        vmem(block, f32),
        vmem((4, 2, parts, 3, cols, depth), f32),
        vmem((4, 2, parts, 3, rows, depth), f32),
        vmem((4, 4, parts, 4, depth), f32),
        vmem((4, 2, parts, 3, rows, depth), f32),
        vmem((4, 4, parts, 4, depth), f32),
        vmem((1, 2, words, 3, cols, depth), i32),
        vmem((1, 2, words, 3, rows, depth), i32),
        vmem((1, 4, words, 4, depth), i32),
        vmem((1, 2, words, 3, rows, depth), i32),
        vmem((1, 4, words, 4, depth), i32),
        vmem((2, 2, depth), f32),
        vmem((2, nx * ny - 1, 2, depth), f32),
        dma((4, 8)),
        dma((4, 8)),
        dma((1, 8)),
        dma((1, 8)),
        dma((2,)),
        dma((2,)),
    ]
    return pl.pallas_call(
        functools.partial(kernel, nx, ny),
        out_shape=[jax.ShapeDtypeStruct(block, f32)] * 2,
        in_specs=[pl.BlockSpec(memory_space=vmem)] * 5,
        out_specs=[pl.BlockSpec(memory_space=vmem)] * 2,
        scratch_shapes=scratch,
        compiler_params=pltpu.CompilerParams(has_side_effects=True, vmem_limit_bytes=48 * 1024 * 1024),
    )(disp, vel, load, flags, mask_bits)


def solution(mesh):
    cells = P(None, "gx", "gy", None)
    return jax.shard_map(
        functools.partial(on_device, mesh.shape["gx"], mesh.shape["gy"]),
        mesh=mesh,
        in_specs=(cells, cells, cells, P("gx", "gy", None), cells),
        out_specs=(cells, cells),
        check_vma=False,
    )
```

time: 620 us -> 77.5 us (0.12); the launches traced: 608 us -> 77.2 us
  blocking collectives: 341 us -> 0 us
  other arithmetic: 105 us -> 0 us
  starting transfers between devices: 103 us -> 0 us
  Pallas kernels: 0 us -> 70.7 us
  waiting for transfers between devices: 42.6 us -> 0 us
  between operations: 14.4 us -> 0.65 us
    psum x8 -> x0, blocking collectives: 341 us -> none  [on_device(): lax.psum((jnp.sum(speed * speed), jnp.sum(speed * (previous - current))),...]
    ppermute x40 -> x0, starting transfers between devices: 103 us -> none  [the longest x20 76.1 us: extended(): lax.ppermute(tail, axis, [(i, (i + 1) % count) for i in range(ends)])]
    another operation x27 -> x0, other arithmetic: 81.3 us -> none  [bond_forces(): return jnp.stack(totals)]
    pallas_call x0 -> x1, Pallas kernels: none -> 70.7 us  [on_device(): pl.pallas_call(functools.partial(kernel, nx, ny), out_shape=[jax.ShapeDty...]
    ppermute x40 -> x0, waiting for transfers between devices: 42.6 us -> none  [the longest x20 29.2 us: extended(): lax.ppermute(head, axis, [((i + 1) % count, i) for i in range(ends)])]
  transfers between devices with their start and end apart: 40 -> 0, of which waited for: 22 -> 0; matrix products, arithmetic and copies ran while one was open for 1% -> 0% of each run, Pallas kernels for 0% -> 0%
where the time goes in v1:
time: 77.5 us; the launch traced here: 77.2 us
  Pallas kernels  70.7 us (91%)
  local copies, waits for them, and re-layouts  5.92 us (8%)
    pallas_call x1, Pallas kernels, on_device(): pl.pallas_call(functools.partial(kernel, nx, ny), out_shape=[jax.ShapeDty...  70.7 us
    unnamed x12, local copies, waits for them, and re-layouts  5.92 us

profile of v1, /device:TPU:0, one launch (start us, length us, event | category | flops | bytes accessed | tf_op | source)
XLA Modules:
  0.0 77.2 jit_solution(1268630567992296506)
XLA Ops:
  0.6 0.0 copy-start
  0.6 0.9 %copy-done = s32[4,8,16,128]{3,2,1,0:T(8,128)S(1)} copy-done((s32[4,8,16,128]{3,2,1,0:T(8,128)S(1)}, s32[4,8,16,128]{3,2,1,0:T(8,128)}, u32[]{:S(2)}) %copy-start) | copy-done | bytes 262168
  1.6 0.0 copy-start.1
  1.6 0.9 %copy-done.1 = f32[3,8,16,128]{3,2,1,0:T(8,128)S(1)} copy-done((f32[3,8,16,128]{3,2,1,0:T(8,128)S(1)}, f32[3,8,16,128]{3,2,1,0:T(8,128)}, u32[]{:S(2)}) %copy-start.1) | copy-done | bytes 196632
  2.5 0.0 copy-start.2
  2.5 0.9 %copy-done.2 = f32[3,8,16,128]{3,2,1,0:T(8,128)S(1)} copy-done((f32[3,8,16,128]{3,2,1,0:T(8,128)S(1)}, f32[3,8,16,128]{3,2,1,0:T(8,128)}, u32[]{:S(2)}) %copy-start.2) | copy-done | bytes 196632
  3.4 0.0 copy-start.3
  3.4 0.9 %copy-done.3 = f32[3,8,16,128]{3,2,1,0:T(8,128)S(1)} copy-done((f32[3,8,16,128]{3,2,1,0:T(8,128)S(1)}, f32[3,8,16,128]{3,2,1,0:T(8,128)}, u32[]{:S(2)}) %copy-start.3) | copy-done | bytes 196632
  4.4 0.0 copy-start.4
  4.4 0.8 %copy-done.4 = s32[8,16,128]{2,1,0:T(8,128)S(1)} copy-done((s32[8,16,128]{2,1,0:T(8,128)S(1)}, s32[8,16,128]{2,1,0:T(8,128)}, u32[]{:S(2)}) %copy-start.4) | copy-done | bytes 65560
  5.2 70.7 %shard_map.68 = (f32[3,8,16,128]{3,2,1,0:T(8,128)S(1)}, f32[3,8,16,128]{3,2,1,0:T(8,128)S(1)}) custom-call(f32[3,8,16,128]{3,2,1,0:T(8,128)S(1)} %copy-done.1, f32[3,8,16,128]{3,2,1,0:T(8,128)S(1)} %copy-done.2, f32[3,8,16,128]{3,2,1,0:T(8,128)S(1)} %copy-done.3, s32[8,16,128]{2,1,0:T(8,128)S(1)} %copy-done.4, s32[4,8,16,128]{3,2,1,0:T(8,128)S(1)} %copy-done), custom_call_target="tpu_custom_call" | custom-call | tf_op jit(solution)/shard_map/pallas_call | solution.py:369
  75.9 0.7 copy.9
  76.6 0.7 copy.10
Async XLA Ops:
  0.6 1.0 %copy-start = (s32[4,8,16,128]{3,2,1,0:T(8,128)S(1)}, s32[4,8,16,128]{3,2,1,0:T(8,128)}, u32[]{:S(2)}) copy-start(s32[4,8,16,128]{3,2,1,0:T(8,128)} %mask.1) | copy-start | bytes 786436
  1.6 0.9 %copy-start.1 = (f32[3,8,16,128]{3,2,1,0:T(8,128)S(1)}, f32[3,8,16,128]{3,2,1,0:T(8,128)}, u32[]{:S(2)}) copy-start(f32[3,8,16,128]{3,2,1,0:T(8,128)} %disp.1) | copy-start | bytes 589828
  2.5 0.9 %copy-start.2 = (f32[3,8,16,128]{3,2,1,0:T(8,128)S(1)}, f32[3,8,16,128]{3,2,1,0:T(8,128)}, u32[]{:S(2)}) copy-start(f32[3,8,16,128]{3,2,1,0:T(8,128)} %vel.1) | copy-start | bytes 589828
  3.4 0.9 %copy-start.3 = (f32[3,8,16,128]{3,2,1,0:T(8,128)S(1)}, f32[3,8,16,128]{3,2,1,0:T(8,128)}, u32[]{:S(2)}) copy-start(f32[3,8,16,128]{3,2,1,0:T(8,128)} %load.1) | copy-start | bytes 589828
  4.4 0.8 %copy-start.4 = (s32[8,16,128]{2,1,0:T(8,128)S(1)}, s32[8,16,128]{2,1,0:T(8,128)}, u32[]{:S(2)}) copy-start(s32[8,16,128]{2,1,0:T(8,128)} %flags.1) | copy-start | bytes 196612
